TPU v7x, 32 devices: a whole 2x2x4 slice. The times are simulated.
32 devices in a mesh: batch: 16 (over z, y, core), gene: 2 (over x).
Axes of the slice: x: 2, y: 2, z: 4, core: 2. Of those that a mesh axis runs over, the one named last changes fastest.
Arguments:
- umi_counts: int32 [16384, 8192], P('batch', 'gene'), may hold values from 0 to 65535
- cell_donors: int32 [16384], P('batch'), may hold values from 0 to 127
- cell_types: int32 [16384], P('batch'), may hold values from 0 to 23
- live_cells: int32 [16], P('batch'), may hold values from 1 to 1024, 10240 in all
- dosages: int32 [128, 2048], P(None, 'batch'), may hold values from 0 to 2
Outputs:
- scores: bfloat16 [24, 8192, 2048], P(None, ('gene', 'batch'))
All inputs are finite; a program needn't handle non-finite values. No bound on the sum of `live_cells` on one device may be relied on, other than what follows from the above.
Results may differ from a plain program's by a relative error of at most 0.0069.
Values may be sent and summed in bfloat16 or wider, within the bound.
A program may use at most 128 MiB of HBM per device.

v0:
```python
import jax
import jax.numpy as jnp
from jax import lax
from jax.sharding import PartitionSpec as P

TYPES = 24
DONORS = 128


def one_hot_rows(group_ids, total_groups):
    columns = jnp.arange(total_groups, dtype=jnp.int32)
    return (group_ids[:, None] == columns[None, :]).astype(jnp.bfloat16)


def standardize_dosage(block_dosage):
    genotype = block_dosage.astype(jnp.float32)
    centred = genotype - jnp.mean(genotype, axis=0, keepdims=True)
    return (centred * lax.rsqrt(jnp.mean(centred * centred, axis=0, keepdims=True) + 1e-06)).astype(
        jnp.bfloat16
    )


def on_device(umi_counts, cell_donors, cell_types, live_cells, dosages):
    total_groups = TYPES * DONORS
    cell_slots = umi_counts.shape[0]
    genes_block = umi_counts.shape[1]
    batch_count = lax.axis_size("batch")
    genes_local = genes_block // batch_count
    slot_index = jnp.arange(cell_slots, dtype=jnp.int32)
    alive_mask = slot_index < live_cells[0]
    cell_group = jnp.where(alive_mask, cell_types * DONORS + cell_donors, -1)
    rounded = umi_counts.astype(jnp.bfloat16)
    exchanged = lax.all_to_all(rounded, "batch", split_axis=1, concat_axis=0, tiled=True)
    all_groups = lax.all_gather(cell_group, "batch", axis=0, tiled=True)
    block_rows = 4 * cell_slots
    block_turns = batch_count // 4

    def add_block(step_index, totals):
        block_counts = lax.dynamic_slice_in_dim(exchanged, step_index * block_rows, block_rows, 0)
        block_groups = lax.dynamic_slice_in_dim(all_groups, step_index * block_rows, block_rows, 0)
        table = one_hot_rows(block_groups, total_groups)
        return totals + lax.dot_general(
            block_counts, table, (((0,), (0,)), ((), ())), preferred_element_type=jnp.float32
        )

    pseudo = lax.fori_loop(
        0, block_turns, add_block, jnp.zeros((genes_local, total_groups), jnp.float32)
    )
    partial_library = jnp.sum(pseudo, axis=0)
    library = jnp.maximum(lax.psum(partial_library, ("batch", "gene")), 1.0)
    logged = jnp.log1p(10000.0 * pseudo / library[None, :]).reshape(genes_local, TYPES, DONORS)
    centred = logged - jnp.mean(logged, axis=2, keepdims=True)
    standard = (
        centred * lax.rsqrt(jnp.mean(centred * centred, axis=2, keepdims=True) + 1e-06)
    ).astype(jnp.bfloat16)
    standard_rows = jnp.transpose(standard, (1, 0, 2)).reshape(TYPES * genes_local, DONORS)
    factor = DONORS ** (-0.5)
    geno_local = standardize_dosage(dosages)
    geno_piece = lax.all_gather(geno_local, "batch", axis=1, tiled=True)
    product = jnp.dot(standard_rows, geno_piece, preferred_element_type=jnp.float32) * factor
    return product.reshape(TYPES, genes_local, geno_piece.shape[1]).astype(jnp.bfloat16)


def solution(mesh):
    placed = (P("batch", "gene"), P("batch"), P("batch"), P("batch"), P(None, "batch"))
    return jax.shard_map(
        on_device,
        mesh=mesh,
        in_specs=placed,
        out_specs=P(None, ("gene", "batch"), None),
        check_vma=False,
    )
```

profile of v0, /device:TPU:14, one launch (start us, length us, event | category | flops | bytes accessed | tf_op | source)
XLA Modules:
  0.0 357.4 jit_solution(3607183109049914522)
XLA Ops:
  0.0 9.0 %convert_element_type.21 = bf16[1024,4096]{1,0:T(8,128)(2,1)} convert(s32[1024,4096]{1,0:T(8,128)} %param.7) | non-fusion elementwise | flops 4194304 | bytes 25165824 | tf_op jit(solution)/shard_map/convert_element_type | solution.py:32
  9.0 7.4 %copy.16 = bf16[128,16,8,256]{3,2,0,1:T(8,128)(2,1)} copy(bf16[128,16,8,256]{3,2,1,0:T(8,128)(2,1)} %bitcast.19) | data formatting | bytes 16777216 | tf_op jit(solution)/shard_map/all_to_all | solution.py:33
  16.5 6.4 %all-to-all-start = ((bf16[1024,16,256]{2,0,1:T(8,128)(2,1)}), bf16[1024,16,256]{2,0,1:T(8,128)(2,1)}, u32[]{:S(2)}, u32[]{:S(2)}) async-start(bf16[1024,16,256]{2,0,1:T(8,128)(2,1)} %bitcast.20), calls=%async_computation | async-start | bytes 16777216 | tf_op jit(solution)/shard_map/all_to_all | solution.py:33
  23.5 0.0 copy-done.2
  23.5 0.0 copy-done.3
  23.5 191.0 %all_gather.6 = s32[16384]{0:T(1024)S(1)} all-gather(s32[1024]{0:T(1024)S(1)} %add_select_fusion), channel_id=1, replica_groups=mesh['batch'=16,'gene'=2] {'batch'}, dimensions={0}, use_global_device_ids=true | all-gather | bytes 69632 | tf_op jit(solution)/shard_map/all_gather | solution.py:34
  214.5 0.0 copy-done.1
  214.6 18.3 %all_gather.7 = bf16[128,2048]{1,0:T(8,128)(2,1)} all-gather(bf16[128,128]{1,0:T(8,128)(2,1)S(1)} %multiply_convert_fusion.2), channel_id=1, replica_groups=mesh['batch'=16,'gene'=2] {'batch'}, dimensions={1}, use_global_device_ids=true | all-gather | bytes 557056 | tf_op jit(solution)/shard_map/all_gather | solution.py:59
  232.9 0.0 all-to-all-done
  232.9 57.8 %while.14 = (s32[]{:T(128)}, f32[256,3072]{1,0:T(8,128)S(1)}, bf16[16384,256]{1,0:T(8,128)(2,1)}, s32[16384]{0:T(1024)S(1)}, s32[]{:T(128)}, /*index=5*/s32[]{:T(128)}, s32[]{:T(128)}, s32[]{:T(128)}) while((s32[]{:T(128)}, f32[256,3072]{1,0:T(8,128)S(1)}, bf16[16384,256]{1,0:T(8,128)(2,1)}, s32[16384]{0:T(1024)S(1)}, s32[]{:T(128)}, ...), condition=%wide.region_1.2_spmd.clone, body=%wide.region_0.1_spmd.clone.sunk | while | flops 6456606720 | bytes 8437917 | solution.py:46
  232.9 14.4 %fusion.11 = f32[256,3072]{1,0:T(8,128)S(1)} fusion(s32[4096]{0:T(1024)S(1)} %dynamic_slice.21, f32[256,3072]{1,0:T(8,128)S(1)} %get-tuple-element.142, bf16[16384,256]{1,0:T(8,128)(2,1)} %get-tuple-element.151, s32[]{:T(128)S(6)} %select_n.16, pred[]{:T(512)S(6)} %compare.3), kind=kOutput, calls=%fused_computation.3.clone.1 | convolution fusion | flops 6456606720 | bytes 8404997 | tf_op jit(solution)/shard_map/while/body/eval_jaxpr/dot_general | solution.py:42
  247.4 14.4 %fusion.11 = f32[256,3072]{1,0:T(8,128)S(1)} fusion(s32[4096]{0:T(1024)S(1)} %dynamic_slice.21, f32[256,3072]{1,0:T(8,128)S(1)} %get-tuple-element.142, bf16[16384,256]{1,0:T(8,128)(2,1)} %get-tuple-element.151, s32[]{:T(128)S(6)} %select_n.16, pred[]{:T(512)S(6)} %compare.3), kind=kOutput, calls=%fused_computation.3.clone.1 | convolution fusion | flops 6456606720 | bytes 8404997 | tf_op jit(solution)/shard_map/while/body/eval_jaxpr/dot_general | solution.py:42
  261.8 14.4 %fusion.11 = f32[256,3072]{1,0:T(8,128)S(1)} fusion(s32[4096]{0:T(1024)S(1)} %dynamic_slice.21, f32[256,3072]{1,0:T(8,128)S(1)} %get-tuple-element.142, bf16[16384,256]{1,0:T(8,128)(2,1)} %get-tuple-element.151, s32[]{:T(128)S(6)} %select_n.16, pred[]{:T(512)S(6)} %compare.3), kind=kOutput, calls=%fused_computation.3.clone.1 | convolution fusion | flops 6456606720 | bytes 8404997 | tf_op jit(solution)/shard_map/while/body/eval_jaxpr/dot_general | solution.py:42
  276.3 14.4 %fusion.11 = f32[256,3072]{1,0:T(8,128)S(1)} fusion(s32[4096]{0:T(1024)S(1)} %dynamic_slice.21, f32[256,3072]{1,0:T(8,128)S(1)} %get-tuple-element.142, bf16[16384,256]{1,0:T(8,128)(2,1)} %get-tuple-element.151, s32[]{:T(128)S(6)} %select_n.16, pred[]{:T(512)S(6)} %compare.3), kind=kOutput, calls=%fused_computation.3.clone.1 | convolution fusion | flops 6456606720 | bytes 8404997 | tf_op jit(solution)/shard_map/while/body/eval_jaxpr/dot_general | solution.py:42
  290.7 2.5 copy.12
  293.3 0.2 reduce_sum.45
  293.4 44.2 %psum.7 = f32[3072]{0:T(1024)S(1)} all-reduce(f32[3072]{0:T(1024)S(1)} %reduce_sum.45), channel_id=1, replica_groups=mesh['batch'=16,'gene'=2] {'batch','gene'}, use_global_device_ids=true, to_apply=%region_3.4 | all-reduce | flops 3072 | bytes 24576 | tf_op jit(solution)/shard_map/psum | solution.py:50
  337.7 3.1 divide_log-plus-one_fusion
  340.8 0.2 reduce_sum.46
  341.1 0.4 multiply_reduce_fusion
  341.5 1.6 fusion.5
  343.1 2.0 copy.13
  345.0 0.0 copy-done
  345.0 12.4 %multiply_convert_fusion = bf16[6144,2048]{1,0:T(8,128)(2,1)} fusion(bf16[6144,128]{1,0:T(8,128)(2,1)S(1)} %bitcast.21, bf16[128,2048]{1,0:T(8,128)(2,1)S(1)} %copy-done), kind=kOutput, calls=%fused_computation.6 | convolution fusion | flops 3246391296 | bytes 27262976 | tf_op jit(solution)/shard_map/dot_general | solution.py:60
  (18 shorter events, 0.2 us)
Async XLA Ops:
  16.5 7.0 %copy-start.2 = (s32[1024]{0:T(1024)S(1)}, s32[1024]{0:T(1024)}, u32[]{:S(2)}) copy-start(s32[1024]{0:T(1024)} %param.8) | copy-start | bytes 12292
  16.5 7.0 %copy-start.3 = (s32[1024]{0:T(1024)S(1)}, s32[1024]{0:T(1024)}, u32[]{:S(2)}) copy-start(s32[1024]{0:T(1024)} %param.9) | copy-start | bytes 12292
  16.5 198.0 %copy-start.1 = (s32[128,128]{1,0:T(8,128)S(1)}, s32[128,128]{1,0:T(8,128)}, u32[]{:S(2)}) copy-start(s32[128,128]{1,0:T(8,128)} %param.11) | copy-start | bytes 196612
  16.5 216.4 %all-to-all-start = ((bf16[1024,16,256]{2,0,1:T(8,128)(2,1)}), bf16[1024,16,256]{2,0,1:T(8,128)(2,1)}, u32[]{:S(2)}, u32[]{:S(2)}) async-start(bf16[1024,16,256]{2,0,1:T(8,128)(2,1)} %bitcast.20), calls=%async_computation | async-start | bytes 16777216 | tf_op jit(solution)/shard_map/all_to_all | solution.py:33
  343.1 2.0 copy-start
where the time goes:
time: 358 us; the launch traced here: 357 us
  blocking collectives  253 us (71%)
  matrix products  70 us (20%)
  other arithmetic  14.7 us (4%)
  local copies, waits for them, and re-layouts  12 us (3%)
  starting transfers between devices  6.37 us (2%)
    all_gather x1, blocking collectives, on_device(): all_groups = lax.all_gather(cell_group, 'batch', axis=0, tiled=True)  191 us
    dot_general x4, matrix products, add_block(): lax.dot_general(block_counts, table, (((0,), (0,)), ((), ())), preferred_...  57.6 us
    psum x1, blocking collectives, on_device(): library = jnp.maximum(lax.psum(partial_library, ('batch', 'gene')), 1.0)  44.2 us
    all_gather x1, blocking collectives, on_device(): geno_piece = lax.all_gather(geno_local, 'batch', axis=1, tiled=True)  18.3 us
    dot_general x1, matrix products, on_device(): jnp.dot(standard_rows, geno_piece, preferred_element_type=jnp.float32)  12.4 us
    convert_element_type x1, other arithmetic, on_device(): rounded = umi_counts.astype(jnp.bfloat16)  9.05 us
    all_to_all x1, local copies, waits for them, and re-layouts, on_device(): lax.all_to_all(rounded, 'batch', split_axis=1, concat_axis=0, tiled=True)  7.43 us
  transfers between devices with their start and end apart: 1, of which 0 were waited for; matrix products, arithmetic and copies ran while one was open for 0% of the time, Pallas kernels for 0%

commit v1 on v0

--- a/solution.py
+++ b/solution.py
@@ -56,7 +56,14 @@
     standard_rows = jnp.transpose(standard, (1, 0, 2)).reshape(TYPES * genes_local, DONORS)
     factor = DONORS ** (-0.5)
     geno_local = standardize_dosage(dosages)
-    geno_piece = lax.all_gather(geno_local, "batch", axis=1, tiled=True)
+    ring = [geno_local]
+    for hop in range(15):
+        ring.append(lax.ppermute(ring[-1], "batch", [(dev, (dev + 1) % 16) for dev in range(16)]))
+    geno_piece = jnp.roll(
+        jnp.concatenate(ring[::-1], axis=1),
+        (lax.axis_index("batch") + 1) * ring[0].shape[1],
+        axis=1,
+    )
     product = jnp.dot(standard_rows, geno_piece, preferred_element_type=jnp.float32) * factor
     return product.reshape(TYPES, genes_local, geno_piece.shape[1]).astype(jnp.bfloat16)
 

time: 358 us -> 432 us (1.21)
  blocking collectives: 253 us -> 56.2 us
  starting transfers between devices: 6.37 us -> 196 us
  waiting for transfers between devices: 0.01 us -> 45.9 us
  local copies, waits for them, and re-layouts: 12 us -> 43 us
    ppermute x0 -> x15, starting transfers between devices: none -> 189 us  [on_device(): lax.ppermute(ring[-1], 'batch', [(dev, (dev + 1) % 16) for dev in range(1...]
    all_gather x1, blocking collectives: 191 us -> 16.1 us  [on_device(): all_groups = lax.all_gather(cell_group, 'batch', axis=0, tiled=True)]
    ppermute x0 -> x15, waiting for transfers between devices: none -> 45.9 us  [on_device(): lax.ppermute(ring[-1], 'batch', [(dev, (dev + 1) % 16) for dev in range(1...]
    unnamed x8 -> x46, local copies, waits for them, and re-layouts: 0.01 us -> 31 us
    all_gather x1 -> x0, blocking collectives: 18.3 us -> none  [on_device(): geno_piece = lax.all_gather(geno_local, 'batch', axis=1, tiled=True)]
  transfers between devices with their start and end apart: 1 -> 16, of which waited for: 0 -> 14; matrix products, arithmetic and copies ran while one was open for 0% -> 7% of each run, Pallas kernels for 0% -> 0%
where the time goes in v1:
time: 432 us; the launch traced here: 429 us
  starting transfers between devices  196 us (45%)
  matrix products  71.1 us (16%)
  blocking collectives  56.2 us (13%)
  waiting for transfers between devices  45.9 us (11%)
  local copies, waits for them, and re-layouts  43 us (10%)
  other arithmetic  15.9 us (4%)
    ppermute x15, starting transfers between devices, on_device(): lax.ppermute(ring[-1], 'batch', [(dev, (dev + 1) % 16) for dev in range(1...  189 us
    dot_general x4, matrix products, add_block(): lax.dot_general(block_counts, table, (((0,), (0,)), ((), ())), preferred_...  57.6 us
    ppermute x15, waiting for transfers between devices, on_device(): lax.ppermute(ring[-1], 'batch', [(dev, (dev + 1) % 16) for dev in range(1...  45.9 us
    psum x1, blocking collectives, on_device(): library = jnp.maximum(lax.psum(partial_library, ('batch', 'gene')), 1.0)  40 us
    unnamed x46, local copies, waits for them, and re-layouts  31 us
    all_gather x1, blocking collectives, on_device(): all_groups = lax.all_gather(cell_group, 'batch', axis=0, tiled=True)  16.1 us
    dot_general x1, matrix products, on_device(): jnp.dot(standard_rows, geno_piece, preferred_element_type=jnp.float32)  13.4 us
    convert_element_type x1, other arithmetic, on_device(): rounded = umi_counts.astype(jnp.bfloat16)  9.05 us
  transfers between devices with their start and end apart: 16, of which 14 were waited for; matrix products, arithmetic and copies ran while one was open for 7% of the time, Pallas kernels for 0%

profile of v1, /device:TPU:14, one launch (start us, length us, event | category | flops | bytes accessed | tf_op | source)
XLA Modules:
  0.0 428.7 jit_solution(10993102229927365934)
XLA Ops:
  0.0 9.0 %convert_element_type.21 = bf16[1024,4096]{1,0:T(8,128)(2,1)} convert(s32[1024,4096]{1,0:T(8,128)} %param.7) | non-fusion elementwise | flops 4194304 | bytes 25165824 | tf_op jit(solution)/shard_map/convert_element_type | solution.py:32
  9.0 7.5 %copy.16 = bf16[128,16,8,256]{3,2,0,1:T(8,128)(2,1)} copy(bf16[128,16,8,256]{3,2,1,0:T(8,128)(2,1)} %bitcast.18) | data formatting | bytes 16777216 | tf_op jit(solution)/shard_map/all_to_all | solution.py:33
  16.5 6.4 %all-to-all-start = ((bf16[1024,16,256]{2,0,1:T(8,128)(2,1)}), bf16[1024,16,256]{2,0,1:T(8,128)(2,1)}, u32[]{:S(2)}, u32[]{:S(2)}) async-start(bf16[1024,16,256]{2,0,1:T(8,128)(2,1)} %bitcast.19), calls=%async_computation | async-start | bytes 16777216 | tf_op jit(solution)/shard_map/all_to_all | solution.py:33
  23.2 35.3 %collective-permute-done = bf16[128,128]{1,0:T(8,128)(2,1)S(1)} collective-permute-done((bf16[128,128]{1,0:T(8,128)(2,1)S(1)}, bf16[128,128]{1,0:T(8,128)(2,1)S(1)}, u32[]{:S(2)}, u32[]{:S(2)}) %collective-permute-start) | collective-permute-done | bytes 32800 | tf_op jit(solution)/shard_map/ppermute | solution.py:61
  58.4 145.2 %collective-permute-start.1 = (bf16[128,128]{1,0:T(8,128)(2,1)S(1)}, bf16[128,128]{1,0:T(8,128)(2,1)S(1)}, u32[]{:S(2)}, u32[]{:S(2)}) collective-permute-start(bf16[128,128]{1,0:T(8,128)(2,1)S(1)} %collective-permute-done), channel_id=1, source_target_pairs={{0,2},{2,4},{4,6},{6,8},{8,10},{10,12},{12,14},{14,16},{16,18},{18... | collective-permute-start | bytes 98312 | tf_op jit(solution)/shard_map/ppermute | solution.py:61
  204.5 3.5 collective-permute-start.2
  208.9 3.4 collective-permute-start.3
  213.2 3.4 collective-permute-start.4
  217.4 3.4 collective-permute-start.5
  221.6 3.4 collective-permute-start.6
  225.9 3.4 collective-permute-start.7
  230.1 3.4 collective-permute-start.8
  234.4 3.4 collective-permute-start.9
  238.6 3.4 collective-permute-start.10
  248.3 3.4 collective-permute-start.12
  253.1 3.4 collective-permute-start.13
  260.8 16.1 %all_gather.3 = s32[16384]{0:T(1024)S(1)} all-gather(s32[1024]{0:T(1024)S(1)} %add_select_fusion), channel_id=1, replica_groups=mesh['batch'=16,'gene'=2] {'batch'}, dimensions={0}, use_global_device_ids=true | all-gather | bytes 69632 | tf_op jit(solution)/shard_map/all_gather | solution.py:34
  307.4 57.8 %while.14 = (s32[]{:T(128)}, f32[256,3072]{1,0:T(8,128)S(1)}, bf16[16384,256]{1,0:T(8,128)(2,1)}, s32[16384]{0:T(1024)S(1)}, s32[]{:T(128)}, /*index=5*/s32[]{:T(128)}, s32[]{:T(128)}, s32[]{:T(128)}) while((s32[]{:T(128)}, f32[256,3072]{1,0:T(8,128)S(1)}, bf16[16384,256]{1,0:T(8,128)(2,1)}, s32[16384]{0:T(1024)S(1)}, s32[]{:T(128)}, ...), condition=%wide.region_1.2_spmd.clone, body=%wide.region_0.1_spmd.clone.sunk | while | flops 6456606720 | bytes 8437917 | solution.py:46
  307.4 14.4 %fusion.12 = f32[256,3072]{1,0:T(8,128)S(1)} fusion(s32[4096]{0:T(1024)S(1)} %dynamic_slice.28, f32[256,3072]{1,0:T(8,128)S(1)} %get-tuple-element.142, bf16[16384,256]{1,0:T(8,128)(2,1)} %get-tuple-element.151, s32[]{:T(128)S(6)} %select_n.31, pred[]{:T(512)S(6)} %compare.4), kind=kOutput, calls=%fused_computation.3.clone.1 | convolution fusion | flops 6456606720 | bytes 8404997 | tf_op jit(solution)/shard_map/while/body/eval_jaxpr/dot_general | solution.py:42
  321.9 14.4 %fusion.12 = f32[256,3072]{1,0:T(8,128)S(1)} fusion(s32[4096]{0:T(1024)S(1)} %dynamic_slice.28, f32[256,3072]{1,0:T(8,128)S(1)} %get-tuple-element.142, bf16[16384,256]{1,0:T(8,128)(2,1)} %get-tuple-element.151, s32[]{:T(128)S(6)} %select_n.31, pred[]{:T(512)S(6)} %compare.4), kind=kOutput, calls=%fused_computation.3.clone.1 | convolution fusion | flops 6456606720 | bytes 8404997 | tf_op jit(solution)/shard_map/while/body/eval_jaxpr/dot_general | solution.py:42
  336.3 14.4 %fusion.12 = f32[256,3072]{1,0:T(8,128)S(1)} fusion(s32[4096]{0:T(1024)S(1)} %dynamic_slice.28, f32[256,3072]{1,0:T(8,128)S(1)} %get-tuple-element.142, bf16[16384,256]{1,0:T(8,128)(2,1)} %get-tuple-element.151, s32[]{:T(128)S(6)} %select_n.31, pred[]{:T(512)S(6)} %compare.4), kind=kOutput, calls=%fused_computation.3.clone.1 | convolution fusion | flops 6456606720 | bytes 8404997 | tf_op jit(solution)/shard_map/while/body/eval_jaxpr/dot_general | solution.py:42
  350.8 14.4 %fusion.12 = f32[256,3072]{1,0:T(8,128)S(1)} fusion(s32[4096]{0:T(1024)S(1)} %dynamic_slice.28, f32[256,3072]{1,0:T(8,128)S(1)} %get-tuple-element.142, bf16[16384,256]{1,0:T(8,128)(2,1)} %get-tuple-element.151, s32[]{:T(128)S(6)} %select_n.31, pred[]{:T(512)S(6)} %compare.4), kind=kOutput, calls=%fused_computation.3.clone.1 | convolution fusion | flops 6456606720 | bytes 8404997 | tf_op jit(solution)/shard_map/while/body/eval_jaxpr/dot_general | solution.py:42
  368.0 40.0 %psum.7 = f32[3072]{0:T(1024)S(1)} all-reduce(f32[3072]{0:T(1024)S(1)} %reduce_sum.45), channel_id=1, replica_groups=mesh['batch'=16,'gene'=2] {'batch','gene'}, use_global_device_ids=true, to_apply=%region_3.4 | all-reduce | flops 3072 | bytes 24576 | tf_op jit(solution)/shard_map/psum | solution.py:50
  415.3 13.4 %multiply_convert_fusion = bf16[6144,2048]{1,0:T(8,128)(2,1)} fusion(bf16[6144,128]{1,0:T(8,128)(2,1)S(1)} %bitcast.20, bf16[128,4096]{1,0:T(8,128)(2,1)} %constant_dynamic-update-slice_fusion, s32[]{:T(128)S(6)} %select_n.27), kind=kOutput, calls=%fused_computation.6 | convolution fusion | flops 3246391296 | bytes 27262980 | tf_op jit(solution)/shard_map/dot_general | solution.py:67
  (87 shorter events, 59.9 us)
Async XLA Ops:
  16.5 6.4 %copy-start = (s32[128,128]{1,0:T(8,128)S(1)}, s32[128,128]{1,0:T(8,128)}, u32[]{:S(2)}) copy-start(s32[128,128]{1,0:T(8,128)} %param.11) | copy-start | bytes 196612
  16.5 244.3 %copy-start.6 = (s32[1024]{0:T(1024)S(1)}, s32[1024]{0:T(1024)}, u32[]{:S(2)}) copy-start(s32[1024]{0:T(1024)} %param.8) | copy-start | bytes 12292
  16.5 244.3 %copy-start.7 = (s32[1024]{0:T(1024)S(1)}, s32[1024]{0:T(1024)}, u32[]{:S(2)}) copy-start(s32[1024]{0:T(1024)} %param.9) | copy-start | bytes 12292
  16.5 290.9 %all-to-all-start = ((bf16[1024,16,256]{2,0,1:T(8,128)(2,1)}), bf16[1024,16,256]{2,0,1:T(8,128)(2,1)}, u32[]{:S(2)}, u32[]{:S(2)}) async-start(bf16[1024,16,256]{2,0,1:T(8,128)(2,1)} %bitcast.19), calls=%async_computation | async-start | bytes 16777216 | tf_op jit(solution)/shard_map/all_to_all | solution.py:33
  23.0 35.4 %collective-permute-start = (bf16[128,128]{1,0:T(8,128)(2,1)S(1)}, bf16[128,128]{1,0:T(8,128)(2,1)S(1)}, u32[]{:S(2)}, u32[]{:S(2)}) collective-permute-start(bf16[128,128]{1,0:T(8,128)(2,1)S(1)} %multiply_convert_fusion.2), channel_id=1, source_target_pairs={{0,2},{2,4},{4,6},{6,8},{8,10},{10,12},{12,14},{14,16},{16,18},{18... | collective-permute-start | bytes 98312 | tf_op jit(solution)/shard_map/ppermute | solution.py:61
  58.4 146.1 %collective-permute-start.1 = (bf16[128,128]{1,0:T(8,128)(2,1)S(1)}, bf16[128,128]{1,0:T(8,128)(2,1)S(1)}, u32[]{:S(2)}, u32[]{:S(2)}) collective-permute-start(bf16[128,128]{1,0:T(8,128)(2,1)S(1)} %collective-permute-done), channel_id=1, source_target_pairs={{0,2},{2,4},{4,6},{6,8},{8,10},{10,12},{12,14},{14,16},{16,18},{18... | collective-permute-start | bytes 98312 | tf_op jit(solution)/shard_map/ppermute | solution.py:61
  204.5 4.4 %collective-permute-start.2 = (bf16[128,128]{1,0:T(8,128)(2,1)S(1)}, bf16[128,128]{1,0:T(8,128)(2,1)S(1)}, u32[]{:S(2)}, u32[]{:S(2)}) collective-permute-start(bf16[128,128]{1,0:T(8,128)(2,1)S(1)} %collective-permute-done.1), channel_id=1, source_target_pairs={{0,2},{2,4},{4,6},{6,8},{8,10},{10,12},{12,14},{14,16},{16,18},{18... | collective-permute-start | bytes 98312 | tf_op jit(solution)/shard_map/ppermute | solution.py:61
  208.9 4.2 collective-permute-start.3
  213.2 4.2 collective-permute-start.4
  217.4 4.2 collective-permute-start.5
  221.6 4.2 collective-permute-start.6
  225.9 4.2 collective-permute-start.7
  230.1 4.2 collective-permute-start.8
  234.4 26.5 %copy-start.1 = (bf16[128,128]{1,0:T(8,128)(2,1)}, bf16[128,128]{1,0:T(8,128)(2,1)S(1)}, u32[]{:S(2)}) copy-start(bf16[128,128]{1,0:T(8,128)(2,1)S(1)} %collective-permute-done.8) | copy-start | bytes 98308
  234.4 4.2 collective-permute-start.9
  238.6 22.2 %copy-start.2 = (bf16[128,128]{1,0:T(8,128)(2,1)}, bf16[128,128]{1,0:T(8,128)(2,1)S(1)}, u32[]{:S(2)}) copy-start(bf16[128,128]{1,0:T(8,128)(2,1)S(1)} %collective-permute-done.9) | copy-start | bytes 98308
  238.6 4.2 collective-permute-start.10
  242.8 0.6 copy-start.3
  243.4 4.2 collective-permute-start.11
  247.7 0.6 copy-start.4
  248.3 4.2 collective-permute-start.12
  252.5 0.6 copy-start.5
  253.1 4.4 %collective-permute-start.13 = (bf16[128,128]{1,0:T(8,128)(2,1)S(1)}, bf16[128,128]{1,0:T(8,128)(2,1)}, u32[]{:S(2)}, u32[]{:S(2)}) collective-permute-start(bf16[128,128]{1,0:T(8,128)(2,1)S(1)} %collective-permute-done.12), channel_id=1, source_target_pairs={{0,2},{2,4},{4,6},{6,8},{8,10},{10,12},{12,14},{14,16},{16,18},{18... | collective-permute-start | bytes 98312 | tf_op jit(solution)/shard_map/ppermute | solution.py:61
  257.5 19.5 %collective-permute-start.14 = (bf16[128,128]{1,0:T(8,128)(2,1)}, bf16[128,128]{1,0:T(8,128)(2,1)}, u32[]{:S(2)}, u32[]{:S(2)}) collective-permute-start(bf16[128,128]{1,0:T(8,128)(2,1)} %collective-permute-done.13), channel_id=1, source_target_pairs={{0,2},{2,4},{4,6},{6,8},{8,10},{10,12},{12,14},{14,16},{16,18},{18... | collective-permute-start | bytes 98312 | tf_op jit(solution)/shard_map/ppermute | solution.py:61
